TPU v7x, 32 devices: a whole 2x2x4 slice. The times are simulated.
32 devices in a mesh: row: 8 (over z, y), col: 4 (over x, core).
Axes of the slice: x: 2, y: 2, z: 4, core: 2. Of those that a mesh axis runs over, the one named last changes fastest.
Arguments:
- points: float32 [16, 4096], P(None, ('col', 'row')), may hold values from -5 to 5
- inv_scales: float32 [16], replicated, may hold values from 0.1 to 0.4
- amplitude: float32 [1], replicated, may hold values from 0.5 to 2
- noise_var: float32 [1], replicated, may hold values from 0.3 to 1
- targets: float32 [8, 4096], P(None, ('col', 'row')), may hold values from -6 to 6
- initial: float32 [8, 4096], P(None, ('col', 'row')), may hold values from -3 to 3
- ritz_basis: float32 [64, 4096], P(None, ('col', 'row')), may hold values from -0.09375 to 0.09375
Outputs:
- solution: float32 [8, 4096], P(None, ('col', 'row'))
- residual: float32 [8, 4096], P(None, ('col', 'row'))
All inputs are finite; a program needn't handle non-finite values.
Results may differ from a plain program's by a relative error of at most 0.00065.
Values sent between devices are 32-bit elements; how exact they have to be, the bound alone decides.
A program may use at most 128 MiB of HBM per device.

v0:
```python
import jax
import jax.numpy as jnp
from jax import lax
from jax.sharding import PartitionSpec as P

ITERS = 1
HIGH = lax.Precision.HIGHEST


def kernel_tile(col_x, col_sq, row_x, row_sq, gain):
    cross_term = jnp.dot(col_x.T, row_x, precision=HIGH, preferred_element_type=jnp.float32)
    distance = jnp.maximum(col_sq[:, None] + row_sq[None, :] - 2.0 * cross_term, 0.0)
    return gain * jnp.exp(-0.5 * distance)


def coarse_solve(factor, rhs_block):
    middle = lax.linalg.triangular_solve(factor, rhs_block, left_side=True, lower=True)
    return lax.linalg.triangular_solve(factor, middle, left_side=True, lower=True, transpose_a=True)


def matmul(left, right):
    return jnp.dot(left, right, precision=HIGH, preferred_element_type=jnp.float32)


def local(points, inv_scales, amplitude, noise_var, targets, initial, ritz_basis):
    gain = amplitude[0]
    nugget = noise_var[0]
    all_x = lax.all_gather(points, ("row", "col"), axis=1, tiled=True) * inv_scales[:, None]
    all_sq = jnp.sum(all_x * all_x, axis=0)
    row_x = points * inv_scales[:, None]
    row_sq = jnp.sum(row_x * row_x, axis=0)

    def apply_operator(vectors):
        partial_value = matmul(
            lax.all_gather(vectors, ("row", "col"), axis=1, tiled=True),
            kernel_tile(all_x, all_sq, row_x, row_sq, gain),
        )
        return partial_value + nugget * vectors

    rhs_count = initial.shape[0]
    applied_all = apply_operator(jnp.concatenate([initial, ritz_basis], 0))
    ritz_image = applied_all[rhs_count:]
    first_residual = targets - applied_all[:rhs_count]
    coarse, projected = lax.psum(
        (matmul(ritz_basis, ritz_image.T), matmul(ritz_basis, first_residual.T)), ("row", "col")
    )
    coarse = 0.5 * (coarse + coarse.T)
    factor = jnp.linalg.cholesky(coarse)
    coarse_inverse = coarse_solve(factor, jnp.eye(coarse.shape[0], dtype=jnp.float32))
    amounts = matmul(coarse_inverse, projected)
    solution = initial + matmul(amounts.T, ritz_basis)
    residual = first_residual - matmul(amounts.T, ritz_image)

    def residual_stats(current):
        return lax.psum(
            (matmul(ritz_image, current.T), jnp.sum(current * current, axis=1)), ("row", "col")
        )

    against, sq_norm = residual_stats(residual)
    direction = residual - matmul(matmul(coarse_inverse, against).T, ritz_basis)

    def plain_step(step, state):
        solution, residual, direction, sq_norm = state
        applied = apply_operator(direction)
        curvature = lax.psum(jnp.sum(direction * applied, axis=1), ("row", "col"))
        step_size = sq_norm / curvature
        solution = solution + step_size[:, None] * direction
        residual = residual - step_size[:, None] * applied
        against, new_norm = residual_stats(residual)
        correction = matmul(matmul(coarse_inverse, against).T, ritz_basis)
        direction = residual + (new_norm / sq_norm)[:, None] * direction - correction
        return (solution, residual, direction, new_norm)

    solution, residual, direction, sq_norm = lax.fori_loop(
        0, ITERS, plain_step, (solution, residual, direction, sq_norm)
    )
    return (solution, residual)


def solution(mesh):
    placed = (
        P(None, ("col", "row")),
        P(),
        P(),
        P(),
        P(None, ("col", "row")),
        P(None, ("col", "row")),
        P(None, ("col", "row")),
    )
    return jax.shard_map(
        local,
        mesh=mesh,
        in_specs=placed,
        out_specs=(P(None, ("col", "row")), P(None, ("col", "row"))),
        check_vma=False,
    )
```

profile of v0, /device:TPU:10, one launch (start us, length us, event | category | flops | bytes accessed | tf_op | source)
XLA Modules:
  0.0 250.7 jit_solution(7430495101600024024)
XLA Ops:
  7.2 0.0 all-gather.2.cloned.1.call-start
  7.2 0.7 constant_dynamic-update-slice_fusion.1
  7.9 0.8 constant_dynamic-update-slice_fusion
  8.7 0.0 copy-start.1
  8.7 0.6 copy-done.1
  9.3 0.0 all-gather.2.cloned.1.call-update
  10.6 0.0 copy-start.2
  10.6 0.8 multiply_reduce_fusion.1
  11.4 31.7 %all_gather.11 = f32[16,4096]{1,0:T(8,128)S(1)} all-gather(f32[16,128]{1,0:T(8,128)} %param.7), channel_id=1, replica_groups=mesh['row'=8,'col'=4] {'row','col'}, dimensions={1}, use_global_device_ids=true | all-gather | bytes 270336 | tf_op jit(solution)/shard_map/all_gather | solution.py:28
  43.1 0.8 multiply_reduce_fusion
  43.9 4.8 %fusion.4 = f32[4096,128]{1,0:T(8,128)S(1)} fusion(f32[128]{0:T(128)S(1)} %multiply_reduce_fusion.1, f32[4096]{0:T(1024)S(1)} %multiply_reduce_fusion, f32[]{:T(128)} %bitcast.38, f32[16,4096]{1,0:T(8,128)S(1)} %all_gather.11, f32[16]{0:T(128)} %param.8, f32[16,128]{1,0:T(8,128)} %param.7), kind=kOutput, calls=%fused_computation.5 | convolution fusion | flops 103876608 | bytes 2384452 | tf_op jit(solution)/shard_map/dot_general | solution.py:11
  48.7 0.0 copy-start
  48.7 0.0 copy-start.3
  48.7 16.1 %all-gather.2.cloned.1.call-done = f32[72,4096]{1,0:T(8,128)} async-done(((f32[72,128]{1,0:T(8,128)}), f32[72,4096]{1,0:T(8,128)}) %all-gather.2.cloned.1.call-update) | async-done | bytes 1179664 | tf_op jit(solution)/shard_map/all_gather | solution.py:35
  64.9 0.0 copy-done.2
  64.9 2.7 %convolution_add_fusion = f32[72,128]{1,0:T(8,128)S(1)} fusion(f32[72,4096]{1,0:T(8,128)} %all-gather.2.cloned.1.call-done, f32[4096,128]{1,0:T(8,128)S(1)} %fusion.4, f32[72,128]{1,0:T(8,128)S(1)} %copy-done.2, f32[]{:T(128)} %bitcast.39), kind=kOutput, calls=%fused_computation.6 | convolution fusion | flops 453003264 | bytes 3350532 | tf_op jit(solution)/shard_map/dot_general | solution.py:22
  67.6 0.0 copy-done
  67.6 0.0 copy-start.4
  67.6 0.2 convolution_bitcast_fusion
  67.8 0.0 copy-done.3
  67.8 0.1 convolution_bitcast_fusion.1
  68.0 40.1 %all-reduce.1 = (f32[64,64]{0,1:T(8,128)S(1)}, f32[64,8]{0,1:T(8,128)S(1)}) all-reduce(f32[64,64]{0,1:T(8,128)S(1)} %convolution_bitcast_fusion, f32[64,8]{0,1:T(8,128)S(1)} %convolution_bitcast_fusion.1), channel_id=1, replica_groups=mesh['row'=8,'col'=4] {'row','col'}, use_global_device_ids=true, to_apply=%region_2.0 | all-reduce | flops 4608 | bytes 36864 | tf_op jit(solution)/shard_map/psum | solution.py:44
  108.1 0.1 copy.9
  108.2 0.1 copy.10
  108.3 5.8 %cholesky.17 = f32[64,64]{1,0:T(8,128)S(1)} custom-call(f32[64,64]{1,0:T(8,128)S(1)} %fusion.13), custom_call_target="Cholesky" | custom-call | tf_op jit(solution)/shard_map/jit(cholesky)/cholesky | solution.py:48
  114.2 0.6 compare_reduce_fusion
  114.8 0.7 fusion.8
  115.5 4.9 %custom-call.8 = f32[1,64,64]{1,2,0:T(8,128)S(1)} custom-call(f32[1,64,64]{2,1,0:T(8,128)S(1)} %fusion.8), custom_call_target="InvertDiagBlocksLowerTriangular" | custom-call | tf_op jit(solution)/shard_map/triangular_solve | solution.py:18
  120.4 0.2 fusion.11
  120.6 0.2 fusion.9
  120.8 0.1 fusion.21
  120.9 0.3 multiply_reduce_fusion.3
  121.2 0.2 fusion.15
  121.4 40.2 %psum.47 = f32[64,8]{1,0:T(8,128)S(1)} all-reduce(f32[64,8]{1,0:T(8,128)S(1)} %fusion.15), channel_id=1, replica_groups=mesh['row'=8,'col'=4] {'row','col'}, use_global_device_ids=true, to_apply=%region_8.0 | all-reduce | flops 512 | bytes 4096 | tf_op jit(solution)/shard_map/psum | solution.py:55
  161.6 0.2 fusion.22
  161.8 0.2 convolution_subtract_fusion
  162.0 30.1 %all_gather.12 = f32[8,4096]{1,0:T(8,128)S(1)} all-gather(f32[8,128]{1,0:T(8,128)S(1)} %convolution_subtract_fusion), channel_id=1, replica_groups=mesh['row'=8,'col'=4] {'row','col'}, dimensions={1}, use_global_device_ids=true | all-gather | bytes 135168 | tf_op jit(solution)/shard_map/while/body/eval_jaxpr/all_gather | solution.py:35
  192.1 1.2 multiply_reduce_fusion.2
  193.3 49.1 %all-reduce = (f32[8]{0:T(128)S(1)}, f32[8]{0:T(128)S(1)}) all-reduce(f32[8]{0:T(128)S(1)} %get-tuple-element.34, f32[8]{0:T(128)S(1)} %get-tuple-element.36), channel_id=1, replica_groups=mesh['row'=8,'col'=4] {'row','col'}, use_global_device_ids=true, to_apply=%region_7.8 | all-reduce | flops 16 | bytes 128 | tf_op jit(solution)/shard_map/psum | solution.py:55
  242.4 0.0 copy-done.4
  242.4 0.7 fusion.5
  243.2 0.7 multiply_subtract_fusion
  (4 shorter events, 0.1 us)
Async XLA Ops:
  7.2 57.7 %all-gather.2.cloned.1.call-start = ((), (), s32[]{:S(2)}) async-start(), calls=%async_computation | async-start | bytes 1216512 | tf_op jit(solution)/shard_map/all_gather | solution.py:35
  8.7 0.6 copy-start.1
  10.6 54.3 %copy-start.2 = (f32[72,128]{1,0:T(8,128)S(1)}, f32[72,128]{1,0:T(8,128)}, u32[]{:S(2)}) copy-start(f32[72,128]{1,0:T(8,128)} %copy-done.1) | copy-start | bytes 110596
  48.7 18.9 %copy-start = (f32[64,128]{1,0:T(8,128)S(1)}, f32[64,128]{1,0:T(8,128)}, u32[]{:S(2)}) copy-start(f32[64,128]{1,0:T(8,128)} %param.13) | copy-start | bytes 98308
  48.7 19.1 %copy-start.3 = (f32[8,128]{1,0:T(8,128)S(1)}, f32[8,128]{1,0:T(8,128)}, u32[]{:S(2)}) copy-start(f32[8,128]{1,0:T(8,128)} %param.11) | copy-start | bytes 12292
  67.6 174.8 %copy-start.4 = (f32[8,128]{1,0:T(8,128)S(1)}, f32[8,128]{1,0:T(8,128)}, u32[]{:S(2)}) copy-start(f32[8,128]{1,0:T(8,128)} %param.12) | copy-start | bytes 12292
Sparse Core Ops, SparseCore 0:
  10.8 53.9 all-gather.1
where the time goes:
time: 251 us
  blocking collectives  191 us (76%)
  waiting for transfers between devices  16.1 us (6%)
  between operations  15.5 us (6%)
  other arithmetic  14.3 us (6%)
  matrix products  11.2 us (4%)
    psum x2, blocking collectives, residual_stats(): lax.psum((matmul(ritz_image, current.T), jnp.sum(current * current, axis=...  89.3 us
    psum x1, blocking collectives, local(): lax.psum((matmul(ritz_basis, ritz_image.T), matmul(ritz_basis, first_resi...  40.1 us
    all_gather x1, blocking collectives, local(): lax.all_gather(points, ('row', 'col'), axis=1, tiled=True)  31.7 us
    all_gather x1, blocking collectives, apply_operator(): lax.all_gather(vectors, ('row', 'col'), axis=1, tiled=True)  30.1 us
    all_gather x1, waiting for transfers between devices, apply_operator(): lax.all_gather(vectors, ('row', 'col'), axis=1, tiled=True)  16.1 us
    another operation x3, other arithmetic, local(): factor = jnp.linalg.cholesky(coarse)  6.52 us
    dot_general x10, matrix products, matmul(): jnp.dot(left, right, precision=HIGH, preferred_element_type=jnp.float32)  5.97 us
    another operation x2, other arithmetic, coarse_solve(): lax.linalg.triangular_solve(factor, middle, left_side=True, lower=True, t...  5.55 us
  transfers between devices with their start and end apart: 1, of which 1 were waited for; matrix products, arithmetic and copies ran while one was open for 3% of the time, Pallas kernels for 0%

commit v1 on v0

--- a/solution.py
+++ b/solution.py
@@ -5,6 +5,10 @@
 
 ITERS = 1
 HIGH = lax.Precision.HIGHEST
+
+
+def sources_all_finish(frame):
+    return jax.lax.psum(jax.lax.psum(frame, "row"), "col")
 
 
 def kernel_tile(col_x, col_sq, row_x, row_sq, gain):
@@ -41,8 +45,8 @@
     applied_all = apply_operator(jnp.concatenate([initial, ritz_basis], 0))
     ritz_image = applied_all[rhs_count:]
     first_residual = targets - applied_all[:rhs_count]
-    coarse, projected = lax.psum(
-        (matmul(ritz_basis, ritz_image.T), matmul(ritz_basis, first_residual.T)), ("row", "col")
+    coarse, projected = sources_all_finish(
+        (matmul(ritz_basis, ritz_image.T), matmul(ritz_basis, first_residual.T))
     )
     coarse = 0.5 * (coarse + coarse.T)
     factor = jnp.linalg.cholesky(coarse)

time: 251 us -> 256 us (1.020)
  blocking collectives: 191 us -> 196 us
    psum x1 -> x2, blocking collectives: 40.1 us -> 43.7 us  [sources_all_finish(): return jax.lax.psum(jax.lax.psum(frame, 'row'), 'col')]
  transfers between devices with their start and end apart: 1 -> 1, of which waited for: 1 -> 1; matrix products, arithmetic and copies ran while one was open for 3% -> 2% of each run, Pallas kernels for 0% -> 0%
where the time goes in v1:
time: 256 us; the launch traced here: 255 us
  blocking collectives  196 us (77%)
  waiting for transfers between devices  16.1 us (6%)
  between operations  15.5 us (6%)
  other arithmetic  14.3 us (6%)
  matrix products  11.2 us (4%)
    psum x2, blocking collectives, residual_stats(): lax.psum((matmul(ritz_image, current.T), jnp.sum(current * current, axis=...  91.1 us
    psum x2, blocking collectives, sources_all_finish(): return jax.lax.psum(jax.lax.psum(frame, 'row'), 'col')  43.7 us
    all_gather x1, blocking collectives, local(): lax.all_gather(points, ('row', 'col'), axis=1, tiled=True)  31.7 us
    all_gather x1, blocking collectives, apply_operator(): lax.all_gather(vectors, ('row', 'col'), axis=1, tiled=True)  29.2 us
    all_gather x1, waiting for transfers between devices, apply_operator(): lax.all_gather(vectors, ('row', 'col'), axis=1, tiled=True)  16.1 us
    another operation x3, other arithmetic, local(): factor = jnp.linalg.cholesky(coarse)  6.52 us
    dot_general x10, matrix products, matmul(): jnp.dot(left, right, precision=HIGH, preferred_element_type=jnp.float32)  5.97 us
    another operation x2, other arithmetic, coarse_solve(): lax.linalg.triangular_solve(factor, middle, left_side=True, lower=True, t...  5.55 us
  transfers between devices with their start and end apart: 1, of which 1 were waited for; matrix products, arithmetic and copies ran while one was open for 2% of the time, Pallas kernels for 0%

profile of v1, /device:TPU:10, one launch (start us, length us, event | category | flops | bytes accessed | tf_op | source)
XLA Modules:
  0.0 255.1 jit_solution(13083647837582029142)
XLA Ops:
  7.2 0.0 all-gather.2.cloned.1.call-start
  7.2 0.7 constant_dynamic-update-slice_fusion.1
  7.9 0.8 constant_dynamic-update-slice_fusion
  8.7 0.0 copy-start.1
  8.7 0.6 copy-done.1
  9.3 0.0 all-gather.2.cloned.1.call-update
  10.6 0.0 copy-start.2
  10.6 0.8 multiply_reduce_fusion.1
  11.4 31.7 %all_gather.11 = f32[16,4096]{1,0:T(8,128)S(1)} all-gather(f32[16,128]{1,0:T(8,128)} %param.7), channel_id=1, replica_groups=mesh['row'=8,'col'=4] {'row','col'}, dimensions={1}, use_global_device_ids=true | all-gather | bytes 270336 | tf_op jit(solution)/shard_map/all_gather | solution.py:32
  43.1 0.8 multiply_reduce_fusion
  43.9 4.8 %fusion.4 = f32[4096,128]{1,0:T(8,128)S(1)} fusion(f32[128]{0:T(128)S(1)} %multiply_reduce_fusion.1, f32[4096]{0:T(1024)S(1)} %multiply_reduce_fusion, f32[]{:T(128)} %bitcast.38, f32[16,4096]{1,0:T(8,128)S(1)} %all_gather.11, f32[16]{0:T(128)} %param.8, f32[16,128]{1,0:T(8,128)} %param.7), kind=kOutput, calls=%fused_computation.5 | convolution fusion | flops 103876608 | bytes 2384452 | tf_op jit(solution)/shard_map/dot_general | solution.py:15
  48.7 0.0 copy-start
  48.7 0.0 copy-start.3
  48.7 16.1 %all-gather.2.cloned.1.call-done = f32[72,4096]{1,0:T(8,128)} async-done(((f32[72,128]{1,0:T(8,128)}), f32[72,4096]{1,0:T(8,128)}) %all-gather.2.cloned.1.call-update) | async-done | bytes 1179664 | tf_op jit(solution)/shard_map/all_gather | solution.py:39
  64.9 0.0 copy-done.2
  64.9 2.7 %convolution_add_fusion = f32[72,128]{1,0:T(8,128)S(1)} fusion(f32[72,4096]{1,0:T(8,128)} %all-gather.2.cloned.1.call-done, f32[4096,128]{1,0:T(8,128)S(1)} %fusion.4, f32[72,128]{1,0:T(8,128)S(1)} %copy-done.2, f32[]{:T(128)} %bitcast.39), kind=kOutput, calls=%fused_computation.6 | convolution fusion | flops 453003264 | bytes 3350532 | tf_op jit(solution)/shard_map/dot_general | solution.py:26
  67.6 0.0 copy-done
  67.6 0.0 copy-start.4
  67.6 0.2 convolution_bitcast_fusion
  67.8 0.0 copy-done.3
  67.8 0.1 convolution_bitcast_fusion.1
  68.0 33.1 %all-reduce.1 = (f32[64,64]{0,1:T(8,128)S(1)}, f32[64,8]{0,1:T(8,128)S(1)}) all-reduce(f32[64,64]{0,1:T(8,128)S(1)} %convolution_bitcast_fusion, f32[64,8]{0,1:T(8,128)S(1)} %convolution_bitcast_fusion.1), channel_id=1, replica_groups=mesh['row'=8,'col'=4] {'row'}, use_global_device_ids=true, to_apply=%region_2.0 | all-reduce | flops 4608 | bytes 36864 | tf_op jit(solution)/shard_map/psum | solution.py:11
  101.1 10.6 %all-reduce.2 = (f32[64,64]{0,1:T(8,128)S(1)}, f32[64,8]{0,1:T(8,128)S(1)}) all-reduce(f32[64,64]{0,1:T(8,128)S(1)} %get-tuple-element.32, f32[64,8]{0,1:T(8,128)S(1)} %get-tuple-element.33), channel_id=1, replica_groups=mesh['row'=8,'col'=4] {'col'}, use_global_device_ids=true, to_apply=%region_3.0 | all-reduce | flops 4608 | bytes 36864 | tf_op jit(solution)/shard_map/psum | solution.py:11
  111.7 0.1 copy.9
  111.8 0.1 copy.10
  111.9 5.8 %cholesky.17 = f32[64,64]{1,0:T(8,128)S(1)} custom-call(f32[64,64]{1,0:T(8,128)S(1)} %fusion.13), custom_call_target="Cholesky" | custom-call | tf_op jit(solution)/shard_map/jit(cholesky)/cholesky | solution.py:52
  117.8 0.6 compare_reduce_fusion
  118.4 0.7 fusion.8
  119.1 4.9 %custom-call.8 = f32[1,64,64]{1,2,0:T(8,128)S(1)} custom-call(f32[1,64,64]{2,1,0:T(8,128)S(1)} %fusion.8), custom_call_target="InvertDiagBlocksLowerTriangular" | custom-call | tf_op jit(solution)/shard_map/triangular_solve | solution.py:22
  124.0 0.2 fusion.11
  124.2 0.2 fusion.9
  124.4 0.1 fusion.21
  124.5 0.3 multiply_reduce_fusion.3
  124.8 0.2 fusion.15
  125.0 41.7 %psum.63 = f32[64,8]{1,0:T(8,128)S(1)} all-reduce(f32[64,8]{1,0:T(8,128)S(1)} %fusion.15), channel_id=1, replica_groups=mesh['row'=8,'col'=4] {'row','col'}, use_global_device_ids=true, to_apply=%region_10.0 | all-reduce | flops 512 | bytes 4096 | tf_op jit(solution)/shard_map/psum | solution.py:59
  166.6 0.2 fusion.22
  166.8 0.2 convolution_subtract_fusion
  167.0 29.2 %all_gather.12 = f32[8,4096]{1,0:T(8,128)S(1)} all-gather(f32[8,128]{1,0:T(8,128)S(1)} %convolution_subtract_fusion), channel_id=1, replica_groups=mesh['row'=8,'col'=4] {'row','col'}, dimensions={1}, use_global_device_ids=true | all-gather | bytes 135168 | tf_op jit(solution)/shard_map/while/body/eval_jaxpr/all_gather | solution.py:39
  196.2 1.2 multiply_reduce_fusion.2
  197.4 49.4 %all-reduce = (f32[8]{0:T(128)S(1)}, f32[8]{0:T(128)S(1)}) all-reduce(f32[8]{0:T(128)S(1)} %get-tuple-element.36, f32[8]{0:T(128)S(1)} %get-tuple-element.38), channel_id=1, replica_groups=mesh['row'=8,'col'=4] {'row','col'}, use_global_device_ids=true, to_apply=%region_9.10 | all-reduce | flops 16 | bytes 128 | tf_op jit(solution)/shard_map/psum | solution.py:59
  246.8 0.0 copy-done.4
  246.8 0.7 fusion.5
  247.6 0.7 multiply_subtract_fusion
  (4 shorter events, 0.1 us)
Async XLA Ops:
  7.2 57.7 %all-gather.2.cloned.1.call-start = ((), (), s32[]{:S(2)}) async-start(), calls=%async_computation | async-start | bytes 1216512 | tf_op jit(solution)/shard_map/all_gather | solution.py:39
  8.7 0.6 copy-start.1
  10.6 54.3 %copy-start.2 = (f32[72,128]{1,0:T(8,128)S(1)}, f32[72,128]{1,0:T(8,128)}, u32[]{:S(2)}) copy-start(f32[72,128]{1,0:T(8,128)} %copy-done.1) | copy-start | bytes 110596
  48.7 18.9 %copy-start = (f32[64,128]{1,0:T(8,128)S(1)}, f32[64,128]{1,0:T(8,128)}, u32[]{:S(2)}) copy-start(f32[64,128]{1,0:T(8,128)} %param.13) | copy-start | bytes 98308
  48.7 19.1 %copy-start.3 = (f32[8,128]{1,0:T(8,128)S(1)}, f32[8,128]{1,0:T(8,128)}, u32[]{:S(2)}) copy-start(f32[8,128]{1,0:T(8,128)} %param.11) | copy-start | bytes 12292
  67.6 179.2 %copy-start.4 = (f32[8,128]{1,0:T(8,128)S(1)}, f32[8,128]{1,0:T(8,128)}, u32[]{:S(2)}) copy-start(f32[8,128]{1,0:T(8,128)} %param.12) | copy-start | bytes 12292
Sparse Core Ops, SparseCore 0:
  10.8 53.9 all-gather.1
